TPU v7x, 32 devices: a whole 2x2x4 slice. The times are simulated.
32 devices in a mesh: dp: 2 (over core), tensor: 16 (over z, y, x).
Axes of the slice: x: 2, y: 2, z: 4, core: 2. Of those that a mesh axis runs over, the one named last changes fastest.
Arguments:
- resid_stream: bfloat16 [512, 4608], P(('dp', 'tensor')), parts along dimension 0, may hold values from -120 to 120, as said below
- pre_gain: float32 [4608], replicated, may hold values from 0.5 to 1.5
- w_gate: bfloat16 [4608, 6144], P(None, 'tensor'), may hold values from -0.09375 to 0.09375
- w_up: bfloat16 [4608, 6144], P(None, 'tensor'), may hold values from -0.09375 to 0.09375
- w_down: bfloat16 [6144, 4608], P('tensor'), may hold values from -0.078125 to 0.078125
- post_gain: float32 [4608], replicated, may hold values from 0.5 to 1.5
Outputs:
- resid_out: bfloat16 [512, 4608], P(('dp', 'tensor')), parts along dimension 0
There are 2 independent parts, one for each index of `dp`. A program takes and returns all parts, laid end to end along the dimension named above; an argument that names none is the same for every part. Nothing has to cross between parts.
Inputs may be any that keep to these rules, and one draw needn't show every extreme that they name: `resid_stream`: entries are real-valued.
All inputs are finite; a program needn't handle non-finite values.
Results may differ from a plain program's by a relative error of at most 0.0029.
Values may be sent and summed in bfloat16 or wider, within the bound.
A program may use at most 128 MiB of HBM per device.

v0:
```python
import jax
import jax.numpy as jnp
from jax import lax
from jax.sharding import PartitionSpec as P

norm_eps = 1e-06


def shards(resid_stream, pre_gain, w_gate, w_up, w_down, post_gain):
    stream = resid_stream.astype(jnp.float32)
    local_norm = stream * lax.rsqrt(jnp.mean(stream * stream, axis=1, keepdims=True) + norm_eps)
    normed = (local_norm * pre_gain).astype(jnp.bfloat16)
    row_piece = lax.all_gather(normed, "tensor", axis=0, tiled=True)
    gate_out = jnp.dot(row_piece, w_gate, preferred_element_type=jnp.float32)
    up_out = jnp.dot(row_piece, w_up, preferred_element_type=jnp.float32)
    hidden = (jax.nn.gelu(gate_out, approximate=True) * up_out).astype(jnp.bfloat16)
    block_rows = lax.psum_scatter(
        jnp.dot(hidden, w_down, preferred_element_type=jnp.float32),
        "tensor",
        scatter_dimension=0,
        tiled=True,
    )
    row_factor = lax.rsqrt(jnp.mean(block_rows * block_rows, axis=1, keepdims=True) + norm_eps)
    post = (block_rows * row_factor * post_gain).astype(jnp.bfloat16)
    post = lax.optimization_barrier(post)
    return (stream + post.astype(jnp.float32)).astype(jnp.bfloat16)


def solution(mesh):
    return jax.shard_map(
        shards,
        mesh=mesh,
        in_specs=(
            P(("dp", "tensor"), None),
            P(),
            P(None, "tensor"),
            P(None, "tensor"),
            P("tensor", None),
            P(),
        ),
        out_specs=P(("dp", "tensor"), None),
        check_vma=False,
    )
```

profile of v0, /device:TPU:0, one launch (start us, length us, event | category | flops | bytes accessed | tf_op | source)
XLA Modules:
  0.0 235.9 jit_solution(629874568969900178)
XLA Ops:
  6.5 0.0 copy-start
  6.5 0.0 all-gather.2.cloned.1.call-start
  6.5 1.2 fusion.10
  7.8 1.7 fusion.12
  9.4 0.0 all-gather.2.cloned.1.call-update
  9.5 0.0 reduce-scatter.2.cloned.1.call-start
  9.5 65.6 %all-gather.2.cloned.1.call-done = bf16[256,4608]{1,0:T(8,128)(2,1)} async-done(((bf16[16,4608]{1,0:T(8,128)(2,1)}), bf16[256,4608]{1,0:T(8,128)(2,1)}) %all-gather.2.cloned.1.call-update) | async-done | bytes 2359312 | tf_op jit(solution)/shard_map/all_gather | solution.py:13
  75.1 4.9 %fusion.22 = f32[256,384]{1,0:T(8,128)} fusion(bf16[256,4608]{1,0:T(8,128)(2,1)} %all-gather.2.cloned.1.call-done, bf16[4608,384]{1,0:T(8,128)(2,1)} %param.8), kind=kOutput, calls=%fused_computation.30 | convolution fusion | flops 905969664 | bytes 6291456 | tf_op jit(solution)/shard_map/dot_general | solution.py:14
  79.9 0.0 copy-done
  79.9 7.6 %fusion.1 = f32[256,4608]{1,0:T(8,128)} fusion(bf16[384,4608]{1,0:T(8,128)(2,1)S(1)} %copy-done, bf16[256,4608]{1,0:T(8,128)(2,1)} %all-gather.2.cloned.1.call-done, bf16[4608,384]{1,0:T(8,128)(2,1)} %param.9, f32[256,384]{1,0:T(8,128)} %fusion.22), kind=kOutput, calls=%fused_computation.2 | convolution fusion | flops 1812922368 | bytes 14548992 | tf_op jit(solution)/shard_map/dot_general | solution.py:18
  87.5 0.0 reduce-scatter.2.cloned.1.call-update
  87.6 137.7 %reduce-scatter.2.cloned.1.call-done = f32[16,4608]{1,0:T(8,128)} async-done(((f32[256,4608]{1,0:T(8,128)}), f32[16,4608]{1,0:T(8,128)}) %reduce-scatter.2.cloned.1.call-update) | async-done | bytes 294928 | tf_op jit(solution)/shard_map/reduce_scatter | solution.py:17
  225.3 1.1 multiply_reduce_fusion
  226.4 1.1 multiply_convert_fusion
  227.5 1.6 fusion.13
  (2 shorter events, 0.0 us)
Async XLA Ops:
  6.5 73.4 %copy-start = (bf16[384,4608]{1,0:T(8,128)(2,1)S(1)}, bf16[384,4608]{1,0:T(8,128)(2,1)}, u32[]{:S(2)}) copy-start(bf16[384,4608]{1,0:T(8,128)(2,1)} %param.10) | copy-start | bytes 10616836
  6.5 68.5 %all-gather.2.cloned.1.call-start = ((), (), s32[]{:S(2)}) async-start(), calls=%async_computation.1 | async-start | bytes 2506752 | tf_op jit(solution)/shard_map/all_gather | solution.py:13
  9.5 215.8 %reduce-scatter.2.cloned.1.call-start = ((), (), s32[]{:S(2)}) async-start(), calls=%async_computation.2 | async-start | bytes 5013504 | tf_op jit(solution)/shard_map/reduce_scatter | solution.py:17
Sparse Core Ops, SparseCore 0:
  10.1 64.9 all-gather.1
  87.7 137.5 reduce-scatter.1
where the time goes:
time: 236 us
  waiting for transfers between devices  203 us (86%)
  between operations  13.4 us (6%)
  matrix products  12.4 us (5%)
  other arithmetic  6.7 us (3%)
    reduce_scatter x1, waiting for transfers between devices, shards(): lax.psum_scatter(jnp.dot(hidden, w_down, preferred_element_type=jnp.float...  138 us
    all_gather x1, waiting for transfers between devices, shards(): row_piece = lax.all_gather(normed, 'tensor', axis=0, tiled=True)  65.6 us
    dot_general x1, matrix products, shards(): jnp.dot(hidden, w_down, preferred_element_type=jnp.float32)  7.59 us
    dot_general x1, matrix products, shards(): gate_out = jnp.dot(row_piece, w_gate, preferred_element_type=jnp.float32)  4.86 us
  transfers between devices with their start and end apart: 2, of which 2 were waited for; matrix products, arithmetic and copies ran while one was open for 0% of the time, Pallas kernels for 0%

commit v1 on v0

--- a/solution.py
+++ b/solution.py
@@ -1,9 +1,17 @@
+import functools
+
 import jax
 import jax.numpy as jnp
 from jax import lax
+from jax.experimental import pallas as pl
+from jax.experimental.pallas import tpu as pltpu
 from jax.sharding import PartitionSpec as P
 
 norm_eps = 1e-06
+SIDE = 2
+PLANE = SIDE * SIDE
+LINE = 4
+MESH = pl.DeviceIdType.MESH
 
 
 def shards(resid_stream, pre_gain, w_gate, w_up, w_down, post_gain):
@@ -26,9 +34,274 @@
     return (stream + post.astype(jnp.float32)).astype(jnp.bfloat16)
 
 
+def tile_of(size, most):
+    return max(t for t in range(128, most + 1, 128) if size % t == 0)
+
+
+def kernel(
+    stream_ref, pre_ref, wg_hbm, wu_hbm, wd_hbm, post_ref, out_ref,
+    w1, w2, gath, gu, hid, part, sendb, rda, rdb, xr, yr, zr,
+    wsem, ssem, agz, agx, agy, agd, rsd, rsx, rsy, rsz,
+):
+    rows, d = stream_ref.shape
+    ff = wg_hbm.shape[1]
+    half = d // 2
+    group = PLANE * rows
+    A, B = pl.ds(0, half), pl.ds(half, half)
+
+    loads = [
+        pltpu.make_async_copy(wg_hbm, w1.at[:, pl.ds(0, ff)], wsem.at[0]),
+        pltpu.make_async_copy(wu_hbm, w1.at[:, pl.ds(ff, ff)], wsem.at[1]),
+        pltpu.make_async_copy(wd_hbm, w2, wsem.at[2]),
+    ]
+    for load in loads:
+        load.start()
+
+    me = lax.axis_index("tensor")
+    x = lax.rem(me, SIDE)
+    y = lax.rem(lax.div(me, SIDE), SIDE)
+    z = lax.div(me, PLANE)
+    spot = lax.rem(me, PLANE)
+    sx = 1 - 2 * x
+    sy = SIDE * (1 - 2 * y)
+    xn, yn = me + sx, me + sy
+    flip = lax.div(z, LINE // 2)
+    p = z + flip * (LINE - 1 - 2 * z)
+    inner = p == 1
+    far = me + PLANE * (1 - 2 * flip)
+    near = me - PLANE * (1 - 2 * flip)
+
+    def plane_of(v):
+        return v + flip * (LINE - 1 - 2 * v)
+
+    order = [plane_of(p), plane_of(1 - p), plane_of(2), plane_of(3)]
+
+    def blk(s, shift):
+        return pl.ds(pl.multiple_of((s * PLANE + spot + shift) * rows, rows), rows)
+
+    pending = []
+
+    def send(src, dst, recv_sem, target, cond=None):
+        copy = pltpu.make_async_remote_copy(
+            src_ref=src, dst_ref=dst, send_sem=ssem.at[len(pending)], recv_sem=recv_sem,
+            device_id={"tensor": target}, device_id_type=MESH,
+        )
+        pending.append((copy, cond))
+        if cond is None:
+            copy.start()
+        else:
+            pl.when(cond)(copy.start)
+
+    def arrive(dst, recv_sem):
+        pltpu.make_async_remote_copy(
+            src_ref=dst, dst_ref=dst, send_sem=ssem.at[0], recv_sem=recv_sem,
+            device_id={"tensor": xn}, device_id_type=MESH,
+        ).wait_recv()
+
+    barrier = pltpu.get_barrier_semaphore()
+    for other in (xn, yn, far):
+        pl.semaphore_signal(barrier, inc=1, device_id={"tensor": other}, device_id_type=MESH)
+
+    @pl.when(inner)
+    def _():
+        pl.semaphore_signal(barrier, inc=1, device_id={"tensor": near}, device_id_type=MESH)
+
+    stream = stream_ref[...].astype(jnp.float32)
+    scale = lax.rsqrt(jnp.mean(stream * stream, axis=1, keepdims=True) + norm_eps)
+    gath[blk(z, 0), :] = (stream * scale * pre_ref[...]).astype(jnp.bfloat16)
+
+    pl.semaphore_wait(barrier, 3 + p)
+
+    def along(k):
+        s = order[k]
+        ref = gath.at[blk(s, 0)]
+        if k > 0:
+            arrive(ref, agz.at[s])
+        if k == 0:
+            send(ref, ref, agz.at[s], far)
+        if k == 1:
+            send(ref, ref, agz.at[s], far, inner)
+        else:
+            send(ref, ref, agz.at[s], near, inner)
+        for cols, kind in ((A, 0), (B, 1)):
+            ref = gath.at[blk(s, 0), cols]
+            send(ref, ref, agx.at[kind, s], xn)
+            other = B if kind == 0 else A
+            ref = gath.at[blk(s, 0), other]
+            send(ref, ref, agy.at[1 - kind, s], yn)
+
+    def across(k):
+        s = order[k]
+        ref = gath.at[blk(s, sx), A]
+        arrive(ref, agx.at[0, s])
+        send(ref, ref, agd.at[0, s], yn)
+        ref = gath.at[blk(s, sy), B]
+        arrive(ref, agy.at[1, s])
+        send(ref, ref, agd.at[1, s], xn)
+
+    tile = tile_of(2 * ff, 256)
+
+    def first_dots(k):
+        s = order[k]
+        arrive(gath.at[blk(s, sx), B], agx.at[1, s])
+        arrive(gath.at[blk(s, sy), A], agy.at[0, s])
+        arrive(gath.at[blk(s, sx + sy), A], agd.at[0, s])
+        arrive(gath.at[blk(s, sx + sy), B], agd.at[1, s])
+        if k == 0:
+            loads[0].wait()
+            loads[1].wait()
+        at = pl.ds(pl.multiple_of(s * group, group), group)
+
+        @pl.loop(0, 2 * ff // tile)
+        def _(i):
+            cols = pl.ds(pl.multiple_of(i * tile, tile), tile)
+            gu[:, cols] = jnp.dot(gath[at, :], w1[:, cols], preferred_element_type=jnp.float32)
+
+        gate, up = gu[:, :ff], gu[:, ff:]
+        hid[at, :] = (jax.nn.gelu(gate, approximate=True) * up).astype(jnp.bfloat16)
+
+    along(0)
+    across(0)
+    along(1)
+    first_dots(0)
+    across(1)
+    along(2)
+    first_dots(1)
+    across(2)
+    along(3)
+    first_dots(2)
+    across(3)
+    first_dots(3)
+
+    back = order[::-1]
+    wide = tile_of(half, 768)
+
+    def last_dot(j):
+        s = back[j]
+        if j == 0:
+            loads[2].wait()
+        at = pl.ds(pl.multiple_of(s * group, group), group)
+
+        @pl.loop(0, d // wide)
+        def _(i):
+            cols = pl.ds(pl.multiple_of(i * wide, wide), wide)
+            res = jnp.dot(hid[at, :], w2[:, cols], preferred_element_type=jnp.float32)
+            part[at, cols] = res
+            sendb[at, cols] = res.astype(jnp.bfloat16)
+
+        send(sendb.at[blk(s, sx + sy), A], rda.at[s], rsd.at[0, s], xn)
+        send(sendb.at[blk(s, sx + sy), B], rdb.at[s], rsd.at[1, s], yn)
+        send(sendb.at[blk(s, sx), A], xr.at[s, :, A], rsx.at[0, s], xn)
+        send(sendb.at[blk(s, sy), B], yr.at[s, :, B], rsy.at[1, s], yn)
+
+    def pass_on(j):
+        s = back[j]
+        arrive(rda.at[s], rsd.at[0, s])
+        at = blk(s, sy)
+        sendb[at, A] = (part[at, A] + rda[s].astype(jnp.float32)).astype(jnp.bfloat16)
+        send(sendb.at[at, A], yr.at[s, :, A], rsy.at[0, s], yn)
+        arrive(rdb.at[s], rsd.at[1, s])
+        at = blk(s, sx)
+        sendb[at, B] = (part[at, B] + rdb[s].astype(jnp.float32)).astype(jnp.bfloat16)
+        send(sendb.at[at, B], xr.at[s, :, B], rsx.at[1, s], xn)
+
+    def settle(j):
+        s = back[j]
+        arrive(xr.at[s, :, A], rsx.at[0, s])
+        arrive(yr.at[s, :, B], rsy.at[1, s])
+        arrive(yr.at[s, :, A], rsy.at[0, s])
+        arrive(xr.at[s, :, B], rsx.at[1, s])
+        at = blk(s, 0)
+        part[at, :] += xr[s].astype(jnp.float32) + yr[s].astype(jnp.float32)
+
+        def add(way):
+            arrive(zr.at[way, s], rsz.at[way, s])
+            part[at, :] += zr[way, s].astype(jnp.float32)
+
+        outward, inward = flip, 1 - flip
+        if j == LINE - 1:
+            add(inward)
+        pl.when(inner)(lambda: add(inward if j == LINE - 2 else outward))
+        if j < LINE - 1:
+            sendb[at, :] = part[at, :].astype(jnp.bfloat16)
+            turn = p if j == LINE - 2 else 0
+            way = flip + turn * (1 - 2 * flip)
+            target = far + turn * (near - far)
+            send(sendb.at[at], zr.at[way, s], rsz.at[way, s], target)
+
+    last_dot(0)
+    last_dot(1)
+    pass_on(0)
+    last_dot(2)
+    pass_on(1)
+    settle(0)
+    last_dot(3)
+    pass_on(2)
+    settle(1)
+    pass_on(3)
+    settle(2)
+    settle(3)
+
+    total = part[blk(z, 0), :]
+    factor = lax.rsqrt(jnp.mean(total * total, axis=1, keepdims=True) + norm_eps)
+    post = (total * factor * post_ref[...]).astype(jnp.bfloat16)
+    stream = stream_ref[...].astype(jnp.float32)
+    out_ref[...] = (stream + post.astype(jnp.float32)).astype(jnp.bfloat16)
+
+    for copy, cond in pending:
+        if cond is None:
+            copy.wait_send()
+        else:
+            pl.when(cond)(copy.wait_send)
+
+
+def fused(resid_stream, pre_gain, w_gate, w_up, w_down, post_gain):
+    rows, d = resid_stream.shape
+    ff = w_gate.shape[1]
+    n = PLANE * LINE
+    bf, f32, dma = jnp.bfloat16, jnp.float32, pltpu.SemaphoreType.DMA
+    vmem = pl.BlockSpec(memory_space=pltpu.VMEM)
+    hbm = pl.BlockSpec(memory_space=pl.ANY)
+    return pl.pallas_call(
+        kernel,
+        out_shape=jax.ShapeDtypeStruct((rows, d), bf),
+        in_specs=[vmem, vmem, hbm, hbm, hbm, vmem],
+        out_specs=vmem,
+        scratch_shapes=[
+            pltpu.VMEM((d, 2 * ff), bf),
+            pltpu.VMEM((ff, d), bf),
+            pltpu.VMEM((n * rows, d), bf),
+            pltpu.VMEM((PLANE * rows, 2 * ff), f32),
+            pltpu.VMEM((n * rows, ff), bf),
+            pltpu.VMEM((n * rows, d), f32),
+            pltpu.VMEM((n * rows, d), bf),
+            pltpu.VMEM((LINE, rows, d // 2), bf),
+            pltpu.VMEM((LINE, rows, d // 2), bf),
+            pltpu.VMEM((LINE, rows, d), bf),
+            pltpu.VMEM((LINE, rows, d), bf),
+            pltpu.VMEM((2, LINE, rows, d), bf),
+            dma((3,)),
+            dma((80,)),
+            dma((LINE,)),
+            dma((2, LINE)),
+            dma((2, LINE)),
+            dma((2, LINE)),
+            dma((2, LINE)),
+            dma((2, LINE)),
+            dma((2, LINE)),
+            dma((2, LINE)),
+        ],
+        compiler_params=pltpu.CompilerParams(
+            collective_id=0, has_side_effects=True, vmem_limit_bytes=60 * 2**20
+        ),
+        name="ffn",
+    )(resid_stream, pre_gain.reshape(1, d), w_gate, w_up, w_down, post_gain.reshape(1, d))
+
+
 def solution(mesh):
+    body = fused if mesh.shape["tensor"] == PLANE * LINE else shards
     return jax.shard_map(
-        shards,
+        body,
         mesh=mesh,
         in_specs=(
             P(("dp", "tensor"), None),

time: 236 us -> 66.9 us (0.28)
  waiting for transfers between devices: 203 us -> 0 us
  Pallas kernels: 0 us -> 62.4 us
  between operations: 13.4 us -> 0.01 us
  matrix products: 12.4 us -> 0 us
  other arithmetic: 6.7 us -> 0 us
  local copies, waits for them, and re-layouts: 0.01 us -> 4.26 us
    reduce_scatter x1 -> x0, waiting for transfers between devices: 138 us -> none  [shards(): lax.psum_scatter(jnp.dot(hidden, w_down, preferred_element_type=jnp.float...]
    all_gather x1 -> x0, waiting for transfers between devices: 65.6 us -> none  [shards(): row_piece = lax.all_gather(normed, 'tensor', axis=0, tiled=True)]
    pallas_call x0 -> x1, Pallas kernels: none -> 62.4 us  [fused(): pl.pallas_call(kernel, out_shape=jax.ShapeDtypeStruct((rows, d), bf), in_...]
    dot_general x2 -> x0, matrix products: 12.4 us -> none  [the longest x1 7.59 us: shards(): jnp.dot(hidden, w_down, preferred_element_type=jnp.float32)]
    convert_element_type x3 -> x0, other arithmetic: 4.36 us -> none  [the longest x1 1.68 us: shards(): normed = (local_norm * pre_gain).astype(jnp.bfloat16)]
    reshape x0 -> x2, local copies, waits for them, and re-layouts: none -> 2.68 us  [the longest x1 1.35 us: fused(): pre_gain.reshape(1, d)]
  transfers between devices with their start and end apart: 2 -> 0, of which waited for: 2 -> 0; matrix products, arithmetic and copies ran while one was open for 0% -> 0% of each run, Pallas kernels for 0% -> 0%
where the time goes in v1:
time: 66.9 us; the launch traced here: 66.7 us
  Pallas kernels  62.4 us (93%)
  local copies, waits for them, and re-layouts  4.26 us (6%)
    pallas_call x1, Pallas kernels, fused(): pl.pallas_call(kernel, out_shape=jax.ShapeDtypeStruct((rows, d), bf), in_...  62.4 us
    unnamed x1, local copies, waits for them, and re-layouts  1.58 us
    reshape x1, local copies, waits for them, and re-layouts, fused(): pre_gain.reshape(1, d)  1.35 us

profile of v1, /device:TPU:0, one launch (start us, length us, event | category | flops | bytes accessed | tf_op | source)
XLA Modules:
  0.0 66.7 jit_solution(10399021774270884946)
XLA Ops:
  0.0 1.3 %reshape.6.pre_ref = f32[1,4608]{1,0:T(1,128)} reshape(f32[4608]{0:T(1024)} %param.7) | data formatting | bytes 36864 | tf_op jit(solution)/shard_map/reshape | solution.py:298
  1.3 1.3 %reshape.7.post_ref = f32[1,4608]{1,0:T(1,128)} reshape(f32[4608]{0:T(1024)} %param.11) | data formatting | bytes 36864 | tf_op jit(solution)/shard_map/reshape | solution.py:298
  2.7 62.4 %ffn.1 = bf16[16,4608]{1,0:T(8,128)(2,1)} custom-call(bf16[16,4608]{1,0:T(8,128)(2,1)} %stream_ref.1, f32[1,4608]{1,0:T(1,128)} %reshape.6.pre_ref, bf16[4608,384]{1,0:T(8,128)(2,1)} %wg_hbm.1, bf16[4608,384]{1,0:T(8,128)(2,1)} %wu_hbm.1, bf16[384,4608]{1,0:T(8,128)(2,1)} %wd_hbm.1, f32[1,4608]{1,0:T(1,128)} %reshape.7.post_ref), custom_call_target="tpu_custom_call" | custom-call | tf_op jit(solution)/shard_map/ffn/pallas_call | solution.py:265
  65.1 1.6 %copy.8 = bf16[16,4608]{1,0:T(8,128)(2,1)} copy(bf16[16,4608]{1,0:T(8,128)(2,1)} %ffn.1) | data formatting | bytes 294912

commit v2 on v1

--- a/solution.py
+++ b/solution.py
@@ -47,15 +47,7 @@
     ff = wg_hbm.shape[1]
     half = d // 2
     group = PLANE * rows
-    A, B = pl.ds(0, half), pl.ds(half, half)
-
-    loads = [
-        pltpu.make_async_copy(wg_hbm, w1.at[:, pl.ds(0, ff)], wsem.at[0]),
-        pltpu.make_async_copy(wu_hbm, w1.at[:, pl.ds(ff, ff)], wsem.at[1]),
-        pltpu.make_async_copy(wd_hbm, w2, wsem.at[2]),
-    ]
-    for load in loads:
-        load.start()
+    A, B = halves = pl.ds(0, half), pl.ds(half, half)
 
     me = lax.axis_index("tensor")
     x = lax.rem(me, SIDE)
@@ -67,10 +59,26 @@
     xn, yn = me + sx, me + sy
     flip = lax.div(z, LINE // 2)
     p = z + flip * (LINE - 1 - 2 * z)
-    inner = p == 1
+    inner, outer = p == 1, p == 0
     far = me + PLANE * (1 - 2 * flip)
     near = me - PLANE * (1 - 2 * flip)
 
+    barrier = pltpu.get_barrier_semaphore()
+    for other in (xn, yn, far):
+        pl.semaphore_signal(barrier, inc=1, device_id={"tensor": other}, device_id_type=MESH)
+
+    @pl.when(inner)
+    def _():
+        pl.semaphore_signal(barrier, inc=1, device_id={"tensor": near}, device_id_type=MESH)
+
+    loads = [
+        pltpu.make_async_copy(wg_hbm, w1.at[:, pl.ds(0, ff)], wsem.at[0]),
+        pltpu.make_async_copy(wu_hbm, w1.at[:, pl.ds(ff, ff)], wsem.at[1]),
+        pltpu.make_async_copy(wd_hbm, w2, wsem.at[2]),
+    ]
+    for load in loads:
+        load.start()
+
     def plane_of(v):
         return v + flip * (LINE - 1 - 2 * v)
 
@@ -81,13 +89,13 @@
 
     pending = []
 
-    def send(src, dst, recv_sem, target, cond=None):
+    def send(src, dst, recv_sem, target, cond=None, inside=False):
         copy = pltpu.make_async_remote_copy(
             src_ref=src, dst_ref=dst, send_sem=ssem.at[len(pending)], recv_sem=recv_sem,
             device_id={"tensor": target}, device_id_type=MESH,
         )
-        pending.append((copy, cond))
-        if cond is None:
+        pending.append(cond)
+        if cond is None or inside:
             copy.start()
         else:
             pl.when(cond)(copy.start)
@@ -98,37 +106,28 @@
             device_id={"tensor": xn}, device_id_type=MESH,
         ).wait_recv()
 
-    barrier = pltpu.get_barrier_semaphore()
-    for other in (xn, yn, far):
-        pl.semaphore_signal(barrier, inc=1, device_id={"tensor": other}, device_id_type=MESH)
-
-    @pl.when(inner)
-    def _():
-        pl.semaphore_signal(barrier, inc=1, device_id={"tensor": near}, device_id_type=MESH)
-
     stream = stream_ref[...].astype(jnp.float32)
     scale = lax.rsqrt(jnp.mean(stream * stream, axis=1, keepdims=True) + norm_eps)
-    gath[blk(z, 0), :] = (stream * scale * pre_ref[...]).astype(jnp.bfloat16)
+    gath[blk(z, 0), :] = (stream * scale * pre_ref[...][None]).astype(jnp.bfloat16)
 
     pl.semaphore_wait(barrier, 3 + p)
 
-    def along(k):
+    def along(k, kind):
         s = order[k]
-        ref = gath.at[blk(s, 0)]
+        ref = gath.at[blk(s, 0), halves[kind]]
         if k > 0:
-            arrive(ref, agz.at[s])
+            arrive(ref, agz.at[kind, s])
         if k == 0:
-            send(ref, ref, agz.at[s], far)
+            send(ref, ref, agz.at[kind, s], far)
         if k == 1:
-            send(ref, ref, agz.at[s], far, inner)
+            send(ref, ref, agz.at[kind, s], far, inner)
         else:
-            send(ref, ref, agz.at[s], near, inner)
-        for cols, kind in ((A, 0), (B, 1)):
-            ref = gath.at[blk(s, 0), cols]
-            send(ref, ref, agx.at[kind, s], xn)
-            other = B if kind == 0 else A
-            ref = gath.at[blk(s, 0), other]
-            send(ref, ref, agy.at[1 - kind, s], yn)
+            send(ref, ref, agz.at[kind, s], near, inner)
+        send(ref, ref, agx.at[kind, s], xn)
+        if kind == 1:
+            send(ref, ref, agy.at[kind, s], yn)
+            ref = gath.at[blk(s, 0), A]
+            send(ref, ref, agy.at[0, s], yn)
 
     def across(k):
         s = order[k]
@@ -160,19 +159,22 @@
         gate, up = gu[:, :ff], gu[:, ff:]
         hid[at, :] = (jax.nn.gelu(gate, approximate=True) * up).astype(jnp.bfloat16)
 
-    along(0)
+    along(0,0)
+    along(0,1)
+    along(1,0)
     across(0)
-    along(1)
+    along(1,1)
+    along(2,0)
+    across(1)
+    along(2,1)
     first_dots(0)
-    across(1)
-    along(2)
+    along(3,0)
+    across(2)
+    along(3,1)
     first_dots(1)
-    across(2)
-    along(3)
+    across(3)
     first_dots(2)
-    across(3)
     first_dots(3)
-
     back = order[::-1]
     wide = tile_of(half, 768)
 
@@ -209,50 +211,80 @@
         s = back[j]
         arrive(xr.at[s, :, A], rsx.at[0, s])
         arrive(yr.at[s, :, B], rsy.at[1, s])
-        arrive(yr.at[s, :, A], rsy.at[0, s])
-        arrive(xr.at[s, :, B], rsx.at[1, s])
         at = blk(s, 0)
-        part[at, :] += xr[s].astype(jnp.float32) + yr[s].astype(jnp.float32)
-
-        def add(way):
-            arrive(zr.at[way, s], rsz.at[way, s])
-            part[at, :] += zr[way, s].astype(jnp.float32)
-
-        outward, inward = flip, 1 - flip
-        if j == LINE - 1:
-            add(inward)
-        pl.when(inner)(lambda: add(inward if j == LINE - 2 else outward))
-        if j < LINE - 1:
-            sendb[at, :] = part[at, :].astype(jnp.bfloat16)
-            turn = p if j == LINE - 2 else 0
-            way = flip + turn * (1 - 2 * flip)
-            target = far + turn * (near - far)
-            send(sendb.at[at], zr.at[way, s], rsz.at[way, s], target)
+        for kind, cols in enumerate(halves):
+            if kind == 0:
+                arrive(yr.at[s, :, A], rsy.at[0, s])
+            else:
+                arrive(xr.at[s, :, B], rsx.at[1, s])
+            total = part[at, cols] + xr[s, :, cols].astype(jnp.float32) + yr[s, :, cols].astype(jnp.float32)
+            part[at, cols] = total
+            if j < LINE - 1:
+                pl.when(outer)(functools.partial(ship, j, kind, far, flip, outer))
+
+    def ship(j, kind, target, way, cond):
+        s = back[j]
+        at = blk(s, 0)
+        sendb[at, halves[kind]] = part[at, halves[kind]].astype(jnp.bfloat16)
+        send(sendb.at[at, halves[kind]], zr.at[way, s, :, halves[kind]], rsz.at[way, kind, s], target, cond, True)
+
+    def add(j, way, kind):
+        s = back[j]
+        at = blk(s, 0)
+        arrive(zr.at[way, s, :, halves[kind]], rsz.at[way, kind, s])
+        part[at, halves[kind]] += zr[way, s, :, halves[kind]].astype(jnp.float32)
+
+    outward, inward = flip, 1 - flip
+
+    def follow(j):
+        @pl.when(inner)
+        def _():
+            for kind in (0, 1):
+                if j == LINE - 2:
+                    add(j, inward, kind)
+                    ship(j, kind, near, inward, inner)
+                else:
+                    add(j, outward, kind)
+                    ship(j, kind, far, outward, inner)
 
     last_dot(0)
     last_dot(1)
     pass_on(0)
     last_dot(2)
     pass_on(1)
+    last_dot(3)
     settle(0)
-    last_dot(3)
     pass_on(2)
+    follow(0)
     settle(1)
     pass_on(3)
+    follow(1)
     settle(2)
+    follow(2)
     settle(3)
+    for kind in (0, 1):
+        add(LINE - 1, inward, kind)
+        pl.when(inner)(functools.partial(add, LINE - 1, outward, kind))
 
     total = part[blk(z, 0), :]
     factor = lax.rsqrt(jnp.mean(total * total, axis=1, keepdims=True) + norm_eps)
-    post = (total * factor * post_ref[...]).astype(jnp.bfloat16)
+    post = (total * factor * post_ref[...][None]).astype(jnp.bfloat16)
     stream = stream_ref[...].astype(jnp.float32)
     out_ref[...] = (stream + post.astype(jnp.float32)).astype(jnp.bfloat16)
 
-    for copy, cond in pending:
+    sent = sendb.at[pl.ds(0, rows), A]
+
+    def drain(i):
+        pltpu.make_async_remote_copy(
+            src_ref=sent, dst_ref=sent, send_sem=ssem.at[i], recv_sem=rsd.at[0, 0],
+            device_id={"tensor": xn}, device_id_type=MESH,
+        ).wait_send()
+
+    for i, cond in enumerate(pending):
         if cond is None:
-            copy.wait_send()
+            drain(i)
         else:
-            pl.when(cond)(copy.wait_send)
+            pl.when(cond)(functools.partial(drain, i))
 
 
 def fused(resid_stream, pre_gain, w_gate, w_up, w_down, post_gain):
@@ -281,21 +313,21 @@
             pltpu.VMEM((LINE, rows, d), bf),
             pltpu.VMEM((2, LINE, rows, d), bf),
             dma((3,)),
-            dma((80,)),
-            dma((LINE,)),
-            dma((2, LINE)),
-            dma((2, LINE)),
-            dma((2, LINE)),
-            dma((2, LINE)),
-            dma((2, LINE)),
-            dma((2, LINE)),
-            dma((2, LINE)),
+            dma((112,)),
+            dma((2, LINE)),
+            dma((2, LINE)),
+            dma((2, LINE)),
+            dma((2, LINE)),
+            dma((2, LINE)),
+            dma((2, LINE)),
+            dma((2, LINE)),
+            dma((2, 2, LINE)),
         ],
         compiler_params=pltpu.CompilerParams(
             collective_id=0, has_side_effects=True, vmem_limit_bytes=60 * 2**20
         ),
         name="ffn",
-    )(resid_stream, pre_gain.reshape(1, d), w_gate, w_up, w_down, post_gain.reshape(1, d))
+    )(resid_stream, pre_gain, w_gate, w_up, w_down, post_gain)
 
 
 def solution(mesh):

time: 66.9 us -> 59.8 us (0.89)
  Pallas kernels: 62.4 us -> 58.1 us
  local copies, waits for them, and re-layouts: 4.26 us -> 1.58 us
    pallas_call x1, Pallas kernels: 62.4 us -> 58.1 us  [fused(): pl.pallas_call(kernel, out_shape=jax.ShapeDtypeStruct((rows, d), bf), in_...]
    reshape x2 -> x0, local copies, waits for them, and re-layouts: 2.68 us -> none  [the longest x1 1.35 us: fused(): pre_gain.reshape(1, d)]
where the time goes in v2:
time: 59.8 us; the launch traced here: 59.7 us
  Pallas kernels  58.1 us (97%)
  local copies, waits for them, and re-layouts  1.58 us (3%)
    pallas_call x1, Pallas kernels, fused(): pl.pallas_call(kernel, out_shape=jax.ShapeDtypeStruct((rows, d), bf), in_...  58.1 us
    unnamed x1, local copies, waits for them, and re-layouts  1.58 us

profile of v2, /device:TPU:0, one launch (start us, length us, event | category | flops | bytes accessed | tf_op | source)
XLA Modules:
  0.0 59.7 jit_solution(12718574144643645597)
XLA Ops:
  0.0 58.1 %ffn.1 = bf16[16,4608]{1,0:T(8,128)(2,1)} custom-call(bf16[16,4608]{1,0:T(8,128)(2,1)} %stream_ref.1, f32[4608]{0:T(1024)} %pre_ref.1, bf16[4608,384]{1,0:T(8,128)(2,1)} %wg_hbm.1, bf16[4608,384]{1,0:T(8,128)(2,1)} %wu_hbm.1, bf16[384,4608]{1,0:T(8,128)(2,1)} %wd_hbm.1, f32[4608]{0:T(1024)} %post_ref.1), custom_call_target="tpu_custom_call" | custom-call | tf_op jit(solution)/shard_map/ffn/pallas_call | solution.py:297
  58.1 1.6 %copy.8 = bf16[16,4608]{1,0:T(8,128)(2,1)} copy(bf16[16,4608]{1,0:T(8,128)(2,1)} %ffn.1) | data formatting | bytes 294912

commit v3 on v2

--- a/solution.py
+++ b/solution.py
@@ -10,6 +10,7 @@
 norm_eps = 1e-06
 SIDE = 2
 PLANE = SIDE * SIDE
+TURNED = 4
 LINE = 4
 MESH = pl.DeviceIdType.MESH
 
@@ -38,16 +39,24 @@
     return max(t for t in range(128, most + 1, 128) if size % t == 0)
 
 
+def cut(d):
+    lanes = d // 128
+    most = 2 * (TURNED * lanes // 36) + lanes % 2
+    return (lanes - most) // 2 * 128, most * 128
+
+
 def kernel(
     stream_ref, pre_ref, wg_hbm, wu_hbm, wd_hbm, post_ref, out_ref,
     w1, w2, gath, gu, hid, part, sendb, rda, rdb, xr, yr, zr,
-    wsem, ssem, agz, agx, agy, agd, rsd, rsx, rsy, rsz,
+    zrc, xyc,
+    wsem, ssem, agz, agx, agy, agd, rsd, rsx, rsy, rsz, agp, agc, rsc, rsp,
 ):
     rows, d = stream_ref.shape
     ff = wg_hbm.shape[1]
-    half = d // 2
+    half, cw = cut(d)
     group = PLANE * rows
     A, B = halves = pl.ds(0, half), pl.ds(half, half)
+    C = pl.ds(2 * half, cw)
 
     me = lax.axis_index("tensor")
     x = lax.rem(me, SIDE)
@@ -56,7 +65,7 @@
     spot = lax.rem(me, PLANE)
     sx = 1 - 2 * x
     sy = SIDE * (1 - 2 * y)
-    xn, yn = me + sx, me + sy
+    xn, yn, dn = me + sx, me + sy, me + sx + sy
     flip = lax.div(z, LINE // 2)
     p = z + flip * (LINE - 1 - 2 * z)
     inner, outer = p == 1, p == 0
@@ -64,7 +73,7 @@
     near = me - PLANE * (1 - 2 * flip)
 
     barrier = pltpu.get_barrier_semaphore()
-    for other in (xn, yn, far):
+    for other in (xn, yn, dn, far):
         pl.semaphore_signal(barrier, inc=1, device_id={"tensor": other}, device_id_type=MESH)
 
     @pl.when(inner)
@@ -94,7 +103,7 @@
             src_ref=src, dst_ref=dst, send_sem=ssem.at[len(pending)], recv_sem=recv_sem,
             device_id={"tensor": target}, device_id_type=MESH,
         )
-        pending.append(cond)
+        pending.append((cond, src.shape))
         if cond is None or inside:
             copy.start()
         else:
@@ -110,7 +119,7 @@
     scale = lax.rsqrt(jnp.mean(stream * stream, axis=1, keepdims=True) + norm_eps)
     gath[blk(z, 0), :] = (stream * scale * pre_ref[...][None]).astype(jnp.bfloat16)
 
-    pl.semaphore_wait(barrier, 3 + p)
+    pl.semaphore_wait(barrier, 4 + p)
 
     def along(k, kind):
         s = order[k]
@@ -138,6 +147,30 @@
         arrive(ref, agy.at[1, s])
         send(ref, ref, agd.at[1, s], xn)
 
+    around = ((sx, xn), (sy, yn), (sx + sy, dn))
+
+    def plane(s):
+        return pl.ds(pl.multiple_of(s * group, group), group)
+
+    def spread():
+        ref = gath.at[blk(z, 0), C]
+        for i, (_, other) in enumerate(around):
+            send(ref, ref, agp.at[i], other)
+
+    def relay(k):
+        s = order[k]
+        ref = gath.at[plane(s), C]
+        if k == 0:
+            for i, (shift, _) in enumerate(around):
+                arrive(gath.at[blk(s, shift), C], agp.at[i])
+            send(ref, ref, agc.at[s], far)
+        else:
+            arrive(ref, agc.at[s])
+        if k == 1:
+            send(ref, ref, agc.at[s], far, inner)
+        else:
+            send(ref, ref, agc.at[s], near, inner)
+
     tile = tile_of(2 * ff, 256)
 
     def first_dots(k):
@@ -159,24 +192,30 @@
         gate, up = gu[:, :ff], gu[:, ff:]
         hid[at, :] = (jax.nn.gelu(gate, approximate=True) * up).astype(jnp.bfloat16)
 
-    along(0,0)
-    along(0,1)
-    along(1,0)
+    spread()
+    along(0, 0)
+    along(0, 1)
+    along(1, 0)
     across(0)
-    along(1,1)
-    along(2,0)
+    along(1, 1)
+    relay(0)
+    along(2, 0)
     across(1)
-    along(2,1)
+    along(2, 1)
     first_dots(0)
-    along(3,0)
+    along(3, 0)
     across(2)
-    along(3,1)
+    along(3, 1)
+    relay(1)
+    relay(2)
+    across(3)
     first_dots(1)
-    across(3)
+    relay(3)
     first_dots(2)
     first_dots(3)
+
     back = order[::-1]
-    wide = tile_of(half, 768)
+    wide = tile_of(d, 768)
 
     def last_dot(j):
         s = back[j]
@@ -247,24 +286,66 @@
                     add(j, outward, kind)
                     ship(j, kind, far, outward, inner)
 
+    def turn(j):
+        s = back[j]
+        send(sendb.at[plane(s), C], zrc.at[flip, s], rsc.at[flip, s], far, outer)
+
+    def add_turned(s, way):
+        arrive(zrc.at[way, s], rsc.at[way, s])
+        part[plane(s), C] += zrc[way, s].astype(jnp.float32)
+
+    def turn_on(j):
+        @pl.when(inner)
+        def _():
+            s = back[j]
+            way, target = (inward, near) if j == LINE - 2 else (outward, far)
+            add_turned(s, way)
+            sendb[plane(s), C] = part[plane(s), C].astype(jnp.bfloat16)
+            send(sendb.at[plane(s), C], zrc.at[way, s], rsc.at[way, s], target, inner, True)
+
+    def share():
+        s = back[LINE - 1]
+        add_turned(s, inward)
+        pl.when(inner)(lambda: add_turned(back[LINE - 1], outward))
+        sendb[plane(s), C] = part[plane(s), C].astype(jnp.bfloat16)
+        for i, (shift, other) in enumerate(around):
+            send(sendb.at[blk(s, shift), C], xyc.at[i], rsp.at[i], other)
+
+    def gain():
+        for i in range(len(around)):
+            arrive(xyc.at[i], rsp.at[i])
+        at = blk(z, 0)
+        part[at, C] += xyc[0].astype(jnp.float32) + xyc[1].astype(jnp.float32) + xyc[2].astype(jnp.float32)
+
+    def close():
+        for kind in (0, 1):
+            add(LINE - 1, inward, kind)
+            pl.when(inner)(functools.partial(add, LINE - 1, outward, kind))
+
     last_dot(0)
+    turn(0)
     last_dot(1)
+    turn(1)
     pass_on(0)
     last_dot(2)
+    turn(2)
     pass_on(1)
+    turn_on(0)
     last_dot(3)
     settle(0)
+    turn_on(1)
     pass_on(2)
     follow(0)
+    turn_on(2)
     settle(1)
     pass_on(3)
     follow(1)
     settle(2)
+    share()
     follow(2)
     settle(3)
-    for kind in (0, 1):
-        add(LINE - 1, inward, kind)
-        pl.when(inner)(functools.partial(add, LINE - 1, outward, kind))
+    close()
+    gain()
 
     total = part[blk(z, 0), :]
     factor = lax.rsqrt(jnp.mean(total * total, axis=1, keepdims=True) + norm_eps)
@@ -272,24 +353,24 @@
     stream = stream_ref[...].astype(jnp.float32)
     out_ref[...] = (stream + post.astype(jnp.float32)).astype(jnp.bfloat16)
 
-    sent = sendb.at[pl.ds(0, rows), A]
-
-    def drain(i):
+    def drain(i, size):
+        sent = sendb.at[pl.ds(0, size[0]), pl.ds(0, size[1])]
         pltpu.make_async_remote_copy(
             src_ref=sent, dst_ref=sent, send_sem=ssem.at[i], recv_sem=rsd.at[0, 0],
             device_id={"tensor": xn}, device_id_type=MESH,
         ).wait_send()
 
-    for i, cond in enumerate(pending):
+    for i, (cond, size) in enumerate(pending):
         if cond is None:
-            drain(i)
+            drain(i, size)
         else:
-            pl.when(cond)(functools.partial(drain, i))
+            pl.when(cond)(functools.partial(drain, i, size))
 
 
 def fused(resid_stream, pre_gain, w_gate, w_up, w_down, post_gain):
     rows, d = resid_stream.shape
     ff = w_gate.shape[1]
+    half, cw = cut(d)
     n = PLANE * LINE
     bf, f32, dma = jnp.bfloat16, jnp.float32, pltpu.SemaphoreType.DMA
     vmem = pl.BlockSpec(memory_space=pltpu.VMEM)
@@ -307,13 +388,15 @@
             pltpu.VMEM((n * rows, ff), bf),
             pltpu.VMEM((n * rows, d), f32),
             pltpu.VMEM((n * rows, d), bf),
-            pltpu.VMEM((LINE, rows, d // 2), bf),
-            pltpu.VMEM((LINE, rows, d // 2), bf),
+            pltpu.VMEM((LINE, rows, half), bf),
+            pltpu.VMEM((LINE, rows, half), bf),
             pltpu.VMEM((LINE, rows, d), bf),
             pltpu.VMEM((LINE, rows, d), bf),
             pltpu.VMEM((2, LINE, rows, d), bf),
+            pltpu.VMEM((2, LINE, PLANE * rows, cw), bf),
+            pltpu.VMEM((3, rows, cw), bf),
             dma((3,)),
-            dma((112,)),
+            dma((144,)),
             dma((2, LINE)),
             dma((2, LINE)),
             dma((2, LINE)),
@@ -322,6 +405,10 @@
             dma((2, LINE)),
             dma((2, LINE)),
             dma((2, 2, LINE)),
+            dma((3,)),
+            dma((LINE,)),
+            dma((2, LINE)),
+            dma((3,)),
         ],
         compiler_params=pltpu.CompilerParams(
             collective_id=0, has_side_effects=True, vmem_limit_bytes=60 * 2**20

time: 59.8 us -> 58 us (0.970)
  Pallas kernels: 58.1 us -> 56.2 us
    pallas_call x1, Pallas kernels: 58.1 us -> 56.2 us  [fused(): pl.pallas_call(kernel, out_shape=jax.ShapeDtypeStruct((rows, d), bf), in_...]
where the time goes in v3:
time: 58 us; the launch traced here: 57.8 us
  Pallas kernels  56.2 us (97%)
  local copies, waits for them, and re-layouts  1.58 us (3%)
    pallas_call x1, Pallas kernels, fused(): pl.pallas_call(kernel, out_shape=jax.ShapeDtypeStruct((rows, d), bf), in_...  56.2 us
    unnamed x1, local copies, waits for them, and re-layouts  1.58 us

profile of v3, /device:TPU:0, one launch (start us, length us, event | category | flops | bytes accessed | tf_op | source)
XLA Modules:
  0.0 57.8 jit_solution(6661662231943653531)
XLA Ops:
  0.0 56.2 %ffn.1 = bf16[16,4608]{1,0:T(8,128)(2,1)} custom-call(bf16[16,4608]{1,0:T(8,128)(2,1)} %stream_ref.1, f32[4608]{0:T(1024)} %pre_ref.1, bf16[4608,384]{1,0:T(8,128)(2,1)} %wg_hbm.1, bf16[4608,384]{1,0:T(8,128)(2,1)} %wu_hbm.1, bf16[384,4608]{1,0:T(8,128)(2,1)} %wd_hbm.1, f32[4608]{0:T(1024)} %post_ref.1), custom_call_target="tpu_custom_call" | custom-call | tf_op jit(solution)/shard_map/ffn/pallas_call | solution.py:378
  56.2 1.6 %copy.8 = bf16[16,4608]{1,0:T(8,128)(2,1)} copy(bf16[16,4608]{1,0:T(8,128)(2,1)} %ffn.1) | data formatting | bytes 294912
